TPU v7x, 32 devices: a whole 2x2x4 slice. The times are simulated.
32 devices in a mesh: dp: 2 (over x), fsdp: 16 (over z, y, core).
Axes of the slice: x: 2, y: 2, z: 4, core: 2. Of those that a mesh axis runs over, the one named last changes fastest.
Arguments:
- small_cols: bfloat16 [24576, 128], P(('dp', 'fsdp')), may hold values from -6 to 6
- wide_cols: bfloat16 [24576, 2, 1536], P(('dp', 'fsdp')), may hold values from -24 to 24
- token_counts: int32 [32], P(('dp', 'fsdp')), may hold values from 144 to 768, as said below
- loss_sums: float32 [32], P(('dp', 'fsdp'))
- weight: float32 [128, 1536], P('fsdp'), may hold values from -0.75 to 0.75
- first_moment: float32 [128, 1536], P('fsdp'), may hold values from -0.002 to 0.002
- second_moment: float32 [128, 1536], P('fsdp'), may hold values from 1e-07 to 1e-06
- step: int32 [], replicated, may hold values from 1 to 2999
Outputs:
- new_weight: float32 [128, 1536], P('fsdp')
- new_first: float32 [128, 1536], P('fsdp')
- new_second: float32 [128, 1536], P('fsdp')
- adam_step: float32 [128, 1536], P('fsdp')
- grad_norm: float32 [], replicated
- mean_loss: float32 [], replicated
Inputs may be any that keep to these rules, and one draw needn't show every extreme that they name: `token_counts`: each count is f * h * w with f from 1 to 3 and h, w from 12 to 16; in every draw some device's count is exactly 768.
All inputs are finite; a program needn't handle non-finite values.
Results may differ from a plain program's by a relative error of at most 0.0003.
Values sent between devices are 32-bit elements; how exact they have to be, the bound alone decides.
A program may use at most 64 MiB of HBM per device.

v0:
```python
import jax
import jax.numpy as jnp
from jax import lax
from jax.sharding import PartitionSpec as P

MAX_NORM = 1.0
BETA_FIRST = 0.9
BETA_SECOND = 0.999
EPSILON_ADAM = 1e-08
LEARN_RATE = 0.02
DECAY_RATE = 0.1


def slot_product(narrow, broad, live_count):
    block_rows = narrow.shape[0]
    half_cols = narrow.shape[1] // 2
    is_live = jnp.arange(block_rows, dtype=jnp.int32) < live_count
    narrow = jnp.where(is_live[:, None], narrow, jnp.zeros_like(narrow))
    portion = jnp.einsum(
        "thc,thd->hcd",
        narrow.reshape(block_rows, 2, half_cols),
        broad,
        preferred_element_type=jnp.float32,
    )
    return portion.reshape(2 * half_cols, broad.shape[2])


def device_term(small_cols, wide_cols, live_count):
    return slot_product(small_cols, wide_cols, live_count)


def on_device(
    small_cols, wide_cols, token_counts, loss_sums, weight, first_moment, second_moment, step
):
    live_count = token_counts[0]
    contribution = device_term(small_cols, wide_cols, live_count)
    count_float = token_counts.astype(jnp.float32)[0]
    loss_local = loss_sums[0]
    owned_sum = lax.psum_scatter(contribution, "fsdp", scatter_dimension=0, tiled=True)
    summed, count_groups, loss_groups = lax.psum((owned_sum, count_float, loss_local), "dp")
    squares, token_total, loss_total = lax.psum(
        (jnp.sum(summed * summed), count_groups, loss_groups), "fsdp"
    )
    gradient = summed / token_total
    grad_norm = jnp.sqrt(squares) / token_total
    mean_loss = loss_total / token_total
    clip_factor = jnp.minimum(1.0, MAX_NORM / (grad_norm + 1e-06))
    clipped = gradient * clip_factor
    new_first = BETA_FIRST * first_moment + (1.0 - BETA_FIRST) * clipped
    new_second = BETA_SECOND * second_moment + (1.0 - BETA_SECOND) * clipped * clipped
    step_float = step.astype(jnp.float32)
    first_hat = new_first / (1.0 - jnp.power(jnp.float32(BETA_FIRST), step_float))
    second_hat = new_second / (1.0 - jnp.power(jnp.float32(BETA_SECOND), step_float))
    adam_step = first_hat / (jnp.sqrt(second_hat) + EPSILON_ADAM) + DECAY_RATE * weight
    new_weight = weight - LEARN_RATE * adam_step
    return (new_weight, new_first, new_second, adam_step, grad_norm, mean_loss)


def solution(mesh):
    in_specs = (
        P(("dp", "fsdp"), None),
        P(("dp", "fsdp"), None, None),
        P(("dp", "fsdp")),
        P(("dp", "fsdp")),
        P("fsdp", None),
        P("fsdp", None),
        P("fsdp", None),
        P(),
    )
    out_specs = (P("fsdp", None), P("fsdp", None), P("fsdp", None), P("fsdp", None), P(), P())
    return jax.shard_map(
        on_device, mesh=mesh, in_specs=in_specs, out_specs=out_specs, check_vma=False
    )
```

profile of v0, /device:TPU:0, one launch (start us, length us, event | category | flops | bytes accessed | tf_op | source)
XLA Modules:
  0.0 127.4 jit_solution(3269646311207091846)
XLA Ops:
  7.2 0.0 copy-start
  7.2 0.0 copy-start.2
  7.2 0.0 copy-start.1
  7.2 0.0 reduce-scatter.2.cloned.1.call-start
  7.9 1.1 copy.16
  9.0 4.2 %fusion = f32[2,64,1536]{2,1,0:T(8,128)} fusion(bf16[768,2,64]{0,2,1:T(8,128)(2,1)S(1)} %bitcast.8, bf16[768,2,1536]{2,1,0:T(2,128)(2,1)} %param.9), kind=kOutput, calls=%fused_computation | convolution fusion | flops 301989888 | bytes 5701632 | tf_op jit(solution)/shard_map/thc,thd->hcd/dot_general | solution.py:19
  13.2 0.0 reduce-scatter.2.cloned.1.call-update
  13.9 58.9 %reduce-scatter.2.cloned.1.call-done = f32[8,1536]{1,0:T(8,128)} async-done(((f32[128,1536]{1,0:T(8,128)}), f32[8,1536]{1,0:T(8,128)}) %reduce-scatter.2.cloned.1.call-update) | async-done | bytes 49168 | tf_op jit(solution)/shard_map/reduce_scatter | solution.py:39
  72.8 10.4 %all-reduce.1 = (f32[8,1536]{1,0:T(8,128)S(1)}, f32[]{:T(128)}, f32[]{:T(128)}) all-reduce(f32[8,1536]{1,0:T(8,128)} %reduce-scatter.2.cloned.1.call-done, f32[]{:T(128)} %bitcast.3, f32[]{:T(128)} %bitcast.4), channel_id=1, replica_groups=mesh['dp'=2,'fsdp'=16] {'dp'}, use_global_device_ids=true, to_apply=%region_1.2 | all-reduce | flops 12290 | bytes 98320 | tf_op jit(solution)/shard_map/psum | solution.py:40
  83.3 0.6 multiply_reduce_fusion
  83.9 30.2 %all-reduce = (f32[]{:T(128)}, f32[]{:T(128)}, f32[]{:T(128)}) all-reduce(f32[]{:T(128)} %multiply_reduce_fusion, f32[]{:T(128)} %get-tuple-element.10, f32[]{:T(128)} %get-tuple-element.11), channel_id=1, replica_groups=mesh['dp'=2,'fsdp'=16] {'fsdp'}, use_global_device_ids=true, to_apply=%region_5.6 | all-reduce | flops 3 | bytes 24 | tf_op jit(solution)/shard_map/psum | solution.py:41
  116.9 0.0 copy-done
  116.9 0.0 copy-done.2
  116.9 0.0 copy-done.1
  116.9 1.4 %multiply_subtract_fusion = (f32[8,1536]{1,0:T(8,128)}, f32[8,1536]{1,0:T(8,128)}, f32[8,1536]{1,0:T(8,128)}, f32[8,1536]{1,0:T(8,128)}) fusion(f32[8,1536]{1,0:T(8,128)S(1)} %copy-done, f32[]{:T(128)S(6)} %sub.10, f32[]{:T(128)S(6)} %sub.9, f32[]{:T(128)S(6)} %min.3, f32[8,1536]{1,0:T(8,128)S(1)} %get-tuple-element.9, f32[]{:T(128)} %get-tuple-element.7, ...), kind=kLoop, calls=%fused_computation.5 | loop fusion | flops 208896 | bytes 393232 | tf_op jit(solution)/shard_map/sub | solution.py:55
  (2 shorter events, 0.0 us)
Async XLA Ops:
  7.2 109.7 %copy-start = (f32[8,1536]{1,0:T(8,128)S(1)}, f32[8,1536]{1,0:T(8,128)}, u32[]{:S(2)}) copy-start(f32[8,1536]{1,0:T(8,128)} %param.12) | copy-start | bytes 147460
  7.2 109.7 %copy-start.2 = (f32[8,1536]{1,0:T(8,128)S(1)}, f32[8,1536]{1,0:T(8,128)}, u32[]{:S(2)}) copy-start(f32[8,1536]{1,0:T(8,128)} %param.13) | copy-start | bytes 147460
  7.2 109.7 %copy-start.1 = (f32[8,1536]{1,0:T(8,128)S(1)}, f32[8,1536]{1,0:T(8,128)}, u32[]{:S(2)}) copy-start(f32[8,1536]{1,0:T(8,128)} %param.14) | copy-start | bytes 147460
  7.2 65.7 %reduce-scatter.2.cloned.1.call-start = ((), (), s32[]{:S(2)}) async-start(), calls=%async_computation.1 | async-start | bytes 835584 | tf_op jit(solution)/shard_map/reduce_scatter | solution.py:39
Sparse Core Ops, SparseCore 0:
  13.3 59.5 reduce-scatter.1
where the time goes:
time: 128 us; the launch traced here: 127 us
  waiting for transfers between devices  59 us (46%)
  blocking collectives  40.6 us (32%)
  between operations  20.6 us (16%)
  matrix products  4.15 us (3%)
  other arithmetic  2.02 us (2%)
    reduce_scatter x1, waiting for transfers between devices, on_device(): lax.psum_scatter(contribution, 'fsdp', scatter_dimension=0, tiled=True)  58.9 us
    psum x1, blocking collectives, on_device(): lax.psum((jnp.sum(summed * summed), count_groups, loss_groups), 'fsdp')  30.2 us
    psum x1, blocking collectives, on_device(): lax.psum((owned_sum, count_float, loss_local), 'dp')  10.4 us
    dot_general x1, matrix products, slot_product(): jnp.einsum('thc,thd->hcd', narrow.reshape(block_rows, 2, half_cols), broa...  4.15 us
  transfers between devices with their start and end apart: 1, of which 1 were waited for; matrix products, arithmetic and copies ran while one was open for 0% of the time, Pallas kernels for 0%

commit v1 on v0

--- a/solution.py
+++ b/solution.py
@@ -1,7 +1,10 @@
 import jax
 import jax.numpy as jnp
 from jax import lax
+from jax.experimental import pallas as pl
+from jax.experimental.pallas import tpu as pltpu
 from jax.sharding import PartitionSpec as P
+import functools
 
 MAX_NORM = 1.0
 BETA_FIRST = 0.9
@@ -56,6 +59,365 @@
     return (new_weight, new_first, new_second, adam_step, grad_norm, mean_loss)
 
 
+CORES = 2
+SIDE = 2
+LANES = 128
+SUBLANES = 8
+WIDTH = 2 * LANES
+AHEAD = 2
+MESH_ID = pl.DeviceIdType.MESH
+
+
+def reduce_kernel(
+    groups,
+    owners,
+    count_ref,
+    loss_ref,
+    narrow_hbm,
+    broad_hbm,
+    clipped_ref,
+    stats_ref,
+    narrow_buf,
+    lhs_buf,
+    broad_buf,
+    own_buf,
+    core_buf,
+    chip_buf,
+    plane_in,
+    plane_sum,
+    line_in,
+    half_sum,
+    half_in,
+    stat_row,
+    stat_in,
+    narrow_sem,
+    broad_sems,
+    core_send,
+    core_recv,
+    plane_send,
+    plane_recv,
+    line_send,
+    line_recv,
+    half_send,
+    half_recv,
+    stat_send,
+    stat_recv,
+):
+    slots, _, width = broad_hbm.shape
+    line = owners // (CORES * SIDE)
+    chunks = width // WIDTH
+    per_half = chunks // groups
+    devices = groups * owners
+    dp = lax.axis_index("dp")
+    place = lax.axis_index("fsdp")
+    core = lax.rem(place, CORES)
+    side = lax.rem(place // CORES, SIDE)
+    level = place // (CORES * SIDE)
+    me = dp * owners + place
+
+    def place_of(level_at, side_at, core_at):
+        return (level_at * SIDE + side_at) * CORES + core_at
+
+    barrier = pltpu.get_barrier_semaphore()
+
+    def greet(step, carry):
+        other = lax.rem(me + step, devices)
+        pl.semaphore_signal(
+            barrier,
+            inc=1,
+            device_id=(other // owners, lax.rem(other, owners)),
+            device_id_type=MESH_ID,
+        )
+        return carry
+
+    lax.fori_loop(1, devices, greet, 0)
+
+    narrow_copy = pltpu.make_async_copy(narrow_hbm, narrow_buf, narrow_sem)
+    narrow_copy.start()
+
+    def broad_copies(step):
+        if step < per_half:
+            chunk = (1 - dp) * per_half + step
+        else:
+            chunk = dp * per_half + step - per_half
+        copies = []
+        for part in range(2):
+            column = pl.multiple_of(chunk * WIDTH + part * LANES, LANES)
+            copies.append(
+                pltpu.make_async_copy(
+                    broad_hbm.at[:, :, pl.ds(column, LANES)],
+                    broad_buf.at[2 * step + part],
+                    broad_sems.at[2 * step + part],
+                )
+            )
+        return copies
+
+    for step in range(AHEAD):
+        for copy in broad_copies(step):
+            copy.start()
+
+    live = count_ref[0]
+    narrow_copy.wait()
+    half_cols = narrow_hbm.shape[1] // 2
+    slot_at = lax.broadcasted_iota(jnp.int32, (LANES, 2 * LANES), 0)
+    pair_at = lax.broadcasted_iota(jnp.int32, (LANES, 2 * LANES), 1)
+    spread = jnp.where(pair_at // 2 == slot_at, 1.0, 0.0).astype(jnp.bfloat16)
+    in_half = lax.rem(pair_at, 2) == slot_at // half_cols
+    for block in range(slots // LANES):
+        doubled = lax.dot_general(
+            narrow_buf[block * LANES : (block + 1) * LANES, :],
+            spread,
+            (((0,), (0,)), ((), ())),
+            preferred_element_type=jnp.float32,
+        )
+        keep = in_half & (block * LANES + pair_at // 2 < live)
+        lhs_buf[:, block * 2 * LANES : (block + 1) * 2 * LANES] = jnp.where(
+            keep, doubled, 0.0
+        ).astype(jnp.bfloat16)
+
+    def core_copy(step):
+        return pltpu.make_async_remote_copy(
+            src_ref=own_buf.at[step, 1 - core],
+            dst_ref=core_buf.at[step],
+            send_sem=core_send.at[step],
+            recv_sem=core_recv.at[step],
+            device_id=(dp, place_of(level, side, 1 - core)),
+            device_id_type=MESH_ID,
+        )
+
+    def plane_copy(slot, item):
+        if slot == 2:
+            source, side_to, dp_to = per_half + item, 1 - side, dp
+        else:
+            source, dp_to = item, 1 - dp
+            side_to = side if slot == 0 else 1 - side
+        return pltpu.make_async_remote_copy(
+            src_ref=chip_buf.at[source, side_to],
+            dst_ref=plane_in.at[slot, item],
+            send_sem=plane_send.at[slot, item],
+            recv_sem=plane_recv.at[slot, item],
+            device_id=(dp_to, place_of(level, side_to, core)),
+            device_id_type=MESH_ID,
+        )
+
+    def line_copy(hop, item):
+        level_to = lax.rem(level + hop, line)
+        return pltpu.make_async_remote_copy(
+            src_ref=plane_sum.at[item, level_to],
+            dst_ref=line_in.at[hop - 1, item],
+            send_sem=line_send.at[hop - 1, item],
+            recv_sem=line_recv.at[hop - 1, item],
+            device_id=(dp, place_of(level_to, side, core)),
+            device_id_type=MESH_ID,
+        )
+
+    def half_copy():
+        return pltpu.make_async_remote_copy(
+            src_ref=half_sum,
+            dst_ref=half_in,
+            send_sem=half_send,
+            recv_sem=half_recv,
+            device_id=(1 - dp, place),
+            device_id_type=MESH_ID,
+        )
+
+    def stat_copy(step):
+        other = lax.rem(me + step, devices)
+        return pltpu.make_async_remote_copy(
+            src_ref=stat_row,
+            dst_ref=stat_in.at[step],
+            send_sem=stat_send.at[step],
+            recv_sem=stat_recv.at[step],
+            device_id=(other // owners, lax.rem(other, owners)),
+            device_id_type=MESH_ID,
+        )
+
+    def across_chip(step):
+        core_copy(step).wait_recv()
+        chip_buf[step] = own_buf[step, core] + core_buf[step]
+        if step < per_half:
+            plane_copy(1, step).start()
+            plane_copy(0, step).start()
+        else:
+            plane_copy(2, step - per_half).start()
+
+    lag = 2
+    for step in range(chunks):
+        if step + AHEAD < chunks:
+            for copy in broad_copies(step + AHEAD):
+                copy.start()
+        for copy in broad_copies(step):
+            copy.wait()
+        block = jnp.concatenate(
+            [
+                broad_buf.at[2 * step + part].reshape(2 * slots, LANES)[...]
+                for part in range(2)
+            ],
+            axis=1,
+        )
+        product = jnp.dot(lhs_buf[...], block, preferred_element_type=jnp.float32)
+        for owner in range(owners):
+            own_buf[
+                step, owner % CORES, owner // CORES % SIDE, owner // (CORES * SIDE)
+            ] = product[owner * SUBLANES : (owner + 1) * SUBLANES, :]
+        if step == 0:
+            pl.semaphore_wait(barrier, devices - 1)
+        core_copy(step).start()
+        if step >= lag:
+            across_chip(step - lag)
+    for step in range(chunks - lag, chunks):
+        across_chip(step)
+
+    for item in range(per_half):
+        for slot in range(3):
+            plane_copy(slot, item).wait_recv()
+        plane_sum[item] = (
+            chip_buf[per_half + item, side]
+            + plane_in[0, item]
+            + plane_in[1, item]
+            + plane_in[2, item]
+        )
+        for hop in range(line - 1, 0, -1):
+            line_copy(hop, item).start()
+
+    squares = jnp.zeros((SUBLANES, WIDTH), jnp.float32)
+    for item in range(per_half):
+        total = plane_sum[item, level]
+        for hop in range(1, line):
+            line_copy(hop, item).wait_recv()
+            total = total + line_in[hop - 1, item]
+        half_sum[item] = total
+        squares = squares + total * total
+    lane = lax.broadcasted_iota(jnp.int32, (1, LANES), 1)
+    row = jnp.where(
+        lane == 0,
+        jnp.sum(squares),
+        jnp.where(
+            lane == 1,
+            live.astype(jnp.float32),
+            jnp.where(lane == 2, loss_ref[0], 0.0),
+        ),
+    )
+    stat_row[...] = row
+    stat_in[0] = row
+
+    def send_stat(step, carry):
+        stat_copy(step).start()
+        return carry
+
+    half_copy().start()
+    lax.fori_loop(1, devices, send_stat, 0)
+
+    def drain_stat(step, carry):
+        stat_copy(step).wait()
+        return carry
+
+    for step in range(chunks):
+        core_copy(step).wait_send()
+    for item in range(per_half):
+        for slot in range(3):
+            plane_copy(slot, item).wait_send()
+        for hop in range(1, line):
+            line_copy(hop, item).wait_send()
+    half_copy().wait()
+    lax.fori_loop(1, devices, drain_stat, 0)
+
+    sums = jnp.sum(stat_in[...], axis=0)
+
+    def entry(index):
+        return jnp.sum(jnp.where(lane == index, sums, 0.0), axis=1, keepdims=True)
+
+    token_total = entry(1)
+    grad_norm = jnp.sqrt(entry(0)) / token_total
+    mean_loss = entry(2) / token_total
+    clip_factor = jnp.minimum(1.0, MAX_NORM / (grad_norm + 1e-06))
+    for item in range(per_half):
+        mine = pl.multiple_of((dp * per_half + item) * WIDTH, WIDTH)
+        other = pl.multiple_of(((1 - dp) * per_half + item) * WIDTH, WIDTH)
+        clipped_ref[:, pl.ds(mine, WIDTH)] = half_sum[item] / token_total * clip_factor
+        clipped_ref[:, pl.ds(other, WIDTH)] = half_in[item] / token_total * clip_factor
+    stats_ref[...] = jnp.where(lane == 0, grad_norm, mean_loss)
+
+
+def reduce_clip(groups, owners, small_cols, wide_cols, token_counts, loss_sums):
+    slots, _, width = wide_cols.shape
+    line = owners // (CORES * SIDE)
+    chunks = width // WIDTH
+    per_half = chunks // groups
+    tile = (SUBLANES, WIDTH)
+    dma = pltpu.SemaphoreType.DMA
+    return pl.pallas_call(
+        functools.partial(reduce_kernel, groups, owners),
+        out_shape=(
+            jax.ShapeDtypeStruct((SUBLANES, width), jnp.float32),
+            jax.ShapeDtypeStruct((1, LANES), jnp.float32),
+        ),
+        in_specs=[
+            pl.BlockSpec(memory_space=pltpu.SMEM),
+            pl.BlockSpec(memory_space=pltpu.SMEM),
+            pl.BlockSpec(memory_space=pl.ANY),
+            pl.BlockSpec(memory_space=pl.ANY),
+        ],
+        out_specs=(
+            pl.BlockSpec(memory_space=pltpu.VMEM),
+            pl.BlockSpec(memory_space=pltpu.VMEM),
+        ),
+        scratch_shapes=[
+            pltpu.VMEM(small_cols.shape, jnp.bfloat16),
+            pltpu.VMEM((small_cols.shape[1], 2 * slots), jnp.bfloat16),
+            pltpu.VMEM((width // LANES, slots, 2, LANES), jnp.bfloat16),
+            pltpu.VMEM((chunks, CORES, SIDE, line) + tile, jnp.float32),
+            pltpu.VMEM((chunks, SIDE, line) + tile, jnp.float32),
+            pltpu.VMEM((chunks, SIDE, line) + tile, jnp.float32),
+            pltpu.VMEM((3, per_half, line) + tile, jnp.float32),
+            pltpu.VMEM((per_half, line) + tile, jnp.float32),
+            pltpu.VMEM((line - 1, per_half) + tile, jnp.float32),
+            pltpu.VMEM((per_half,) + tile, jnp.float32),
+            pltpu.VMEM((per_half,) + tile, jnp.float32),
+            pltpu.VMEM((1, LANES), jnp.float32),
+            pltpu.VMEM((groups * owners, 1, LANES), jnp.float32),
+            dma,
+            dma((width // LANES,)),
+            dma((chunks,)),
+            dma((chunks,)),
+            dma((3, per_half)),
+            dma((3, per_half)),
+            dma((line - 1, per_half)),
+            dma((line - 1, per_half)),
+            dma,
+            dma,
+            dma((groups * owners,)),
+            dma((groups * owners,)),
+        ],
+        compiler_params=pltpu.CompilerParams(collective_id=0, has_side_effects=True),
+    )(token_counts, loss_sums, small_cols, wide_cols)
+
+
+def on_device_kernel(
+    groups,
+    owners,
+    small_cols,
+    wide_cols,
+    token_counts,
+    loss_sums,
+    weight,
+    first_moment,
+    second_moment,
+    step,
+):
+    clipped, stats = reduce_clip(
+        groups, owners, small_cols, wide_cols, token_counts, loss_sums
+    )
+    new_first = BETA_FIRST * first_moment + (1.0 - BETA_FIRST) * clipped
+    new_second = BETA_SECOND * second_moment + (1.0 - BETA_SECOND) * clipped * clipped
+    step_float = step.astype(jnp.float32)
+    first_hat = new_first / (1.0 - jnp.power(jnp.float32(BETA_FIRST), step_float))
+    second_hat = new_second / (1.0 - jnp.power(jnp.float32(BETA_SECOND), step_float))
+    adam_step = first_hat / (jnp.sqrt(second_hat) + EPSILON_ADAM) + DECAY_RATE * weight
+    new_weight = weight - LEARN_RATE * adam_step
+    return (new_weight, new_first, new_second, adam_step, stats[0, 0], stats[0, 1])
+
+
 def solution(mesh):
     in_specs = (
         P(("dp", "fsdp"), None),
@@ -68,6 +430,14 @@
         P(),
     )
     out_specs = (P("fsdp", None), P("fsdp", None), P("fsdp", None), P("fsdp", None), P(), P())
-    return jax.shard_map(
-        on_device, mesh=mesh, in_specs=in_specs, out_specs=out_specs, check_vma=False
-    )
+    groups, owners = mesh.shape["dp"], mesh.shape["fsdp"]
+
+    def step_fn(small_cols, *rest):
+        rows = small_cols.shape[1]
+        fits = groups == SIDE and owners * SUBLANES == rows
+        body = functools.partial(on_device_kernel, groups, owners) if fits else on_device
+        return jax.shard_map(
+            body, mesh=mesh, in_specs=in_specs, out_specs=out_specs, check_vma=False
+        )(small_cols, *rest)
+
+    return step_fn

time: 128 us -> 31.2 us (0.24)
  waiting for transfers between devices: 59 us -> 0 us
  blocking collectives: 40.6 us -> 0 us
  Pallas kernels: 0 us -> 25.3 us
  between operations: 20.6 us -> 2.74 us
  matrix products: 4.15 us -> 0 us
    reduce_scatter x1 -> x0, waiting for transfers between devices: 58.9 us -> none  [on_device(): lax.psum_scatter(contribution, 'fsdp', scatter_dimension=0, tiled=True)]
    psum x2 -> x0, blocking collectives: 40.6 us -> none  [the longest x1 30.2 us: on_device(): lax.psum((jnp.sum(summed * summed), count_groups, loss_groups), 'fsdp')]
    pallas_call x0 -> x1, Pallas kernels: none -> 25.3 us  [reduce_clip(): pl.pallas_call(functools.partial(reduce_kernel, groups, owners), out_shap...]
    dot_general x1 -> x0, matrix products: 4.15 us -> none  [slot_product(): jnp.einsum('thc,thd->hcd', narrow.reshape(block_rows, 2, half_cols), broa...]
    slice x0 -> x1, local copies, waits for them, and re-layouts: none -> 1.32 us  [on_device_kernel(): stats[0, 1]]
  transfers between devices with their start and end apart: 1 -> 0, of which waited for: 1 -> 0; matrix products, arithmetic and copies ran while one was open for 0% -> 0% of each run, Pallas kernels for 0% -> 0%
where the time goes in v1:
time: 31.2 us; the launch traced here: 30.9 us
  Pallas kernels  25.3 us (81%)
  between operations  2.74 us (9%)
  other arithmetic  1.49 us (5%)
  local copies, waits for them, and re-layouts  1.34 us (4%)
    pallas_call x1, Pallas kernels, reduce_clip(): pl.pallas_call(functools.partial(reduce_kernel, groups, owners), out_shap...  25.3 us
    sub x1, other arithmetic, on_device_kernel(): new_weight = weight - LEARN_RATE * adam_step  1.49 us
    slice x1, local copies, waits for them, and re-layouts, on_device_kernel(): stats[0, 1]  1.32 us

profile of v1, /device:TPU:0, one launch (start us, length us, event | category | flops | bytes accessed | tf_op | source)
XLA Modules:
  0.0 30.9 jit_solution(1659945879556684631)
XLA Ops:
  0.6 0.0 copy-start
  0.6 0.0 copy-start.2
  0.7 0.0 copy-start.1
  2.0 25.3 %shard_map.127 = (f32[8,1536]{1,0:T(8,128)}, f32[1,128]{1,0:T(1,128)}) custom-call(s32[1]{0:T(128)S(6)} %copy.14.count_ref, f32[1]{0:T(128)S(6)} %copy.15.loss_ref, bf16[768,128]{1,0:T(8,128)(2,1)} %narrow_hbm.1, bf16[768,2,1536]{2,1,0:T(2,128)(2,1)} %broad_hbm.1), custom_call_target="tpu_custom_call" | custom-call | tf_op jit(solution)/shard_map/pallas_call | solution.py:349
  28.0 0.0 copy-done
  28.0 0.0 copy-done.2
  28.0 0.0 copy-done.1
  28.1 1.5 %multiply_subtract_fusion = (f32[8,1536]{1,0:T(8,128)}, f32[8,1536]{1,0:T(8,128)}, f32[8,1536]{1,0:T(8,128)}, f32[8,1536]{1,0:T(8,128)}) fusion(f32[8,1536]{1,0:T(8,128)S(1)} %copy-done, f32[]{:T(128)S(6)} %sub.10, f32[]{:T(128)S(6)} %sub.9, f32[8,1536]{1,0:T(8,128)} %get-tuple-element.8, f32[8,1536]{1,0:T(8,128)S(1)} %copy-done.1, f32[8,1536]{1,0:T(8,128)S(1)} %copy-done.2), kind=kLoop, calls=%fused_computation.2 | loop fusion | flops 184320 | bytes 393224 | tf_op jit(solution)/shard_map/sub | solution.py:417
  29.5 1.3 %fusion.2 = (f32[1,1]{1,0:T(1,128)}, f32[1,1]{1,0:T(1,128)}) fusion(f32[1,128]{1,0:T(1,128)} %get-tuple-element.9), kind=kLoop, calls=%fused_computation.5 | loop fusion | bytes 16 | tf_op jit(solution)/shard_map/slice | solution.py:418
Async XLA Ops:
  0.6 27.4 %copy-start = (f32[8,1536]{1,0:T(8,128)S(1)}, f32[8,1536]{1,0:T(8,128)}, u32[]{:S(2)}) copy-start(f32[8,1536]{1,0:T(8,128)} %param.12) | copy-start | bytes 147460
  0.6 27.4 %copy-start.2 = (f32[8,1536]{1,0:T(8,128)S(1)}, f32[8,1536]{1,0:T(8,128)}, u32[]{:S(2)}) copy-start(f32[8,1536]{1,0:T(8,128)} %param.13) | copy-start | bytes 147460
  0.7 27.4 %copy-start.1 = (f32[8,1536]{1,0:T(8,128)S(1)}, f32[8,1536]{1,0:T(8,128)}, u32[]{:S(2)}) copy-start(f32[8,1536]{1,0:T(8,128)} %param.14) | copy-start | bytes 147460

commit v2 on v1

--- a/solution.py
+++ b/solution.py
@@ -65,18 +65,43 @@
 SUBLANES = 8
 WIDTH = 2 * LANES
 AHEAD = 2
+STEP_BITS = 16
 MESH_ID = pl.DeviceIdType.MESH
+
+
+def complement_power(base, exponent):
+    square = 1.0 - jnp.float32(base)
+    total = jnp.float32(0.0)
+    for bit in range(STEP_BITS):
+        taken = (exponent // (1 << bit)) % 2 == 1
+        total = jnp.where(taken, total + square - total * square, total)
+        square = square * (2.0 - square)
+    return total
 
 
 def reduce_kernel(
     groups,
     owners,
+    narrow_hbm,
+    broad_hbm,
+    count_hbm,
+    loss_hbm,
+    weight_hbm,
+    first_hbm,
+    second_hbm,
+    step_hbm,
+    weight_out,
+    first_out,
+    second_out,
+    adam_out,
+    norm_out,
+    loss_out,
     count_ref,
     loss_ref,
-    narrow_hbm,
-    broad_hbm,
-    clipped_ref,
-    stats_ref,
+    step_ref,
+    weight_buf,
+    first_buf,
+    second_buf,
     narrow_buf,
     lhs_buf,
     broad_buf,
@@ -90,7 +115,7 @@
     half_in,
     stat_row,
     stat_in,
-    narrow_sem,
+    small_sems,
     broad_sems,
     core_send,
     core_recv,
@@ -120,20 +145,30 @@
 
     barrier = pltpu.get_barrier_semaphore()
 
-    def greet(step, carry):
-        other = lax.rem(me + step, devices)
+    partners = [(dp, place_of(level, side, 1 - core))]
+    partners += [
+        (1 - dp, place),
+        (1 - dp, place_of(level, 1 - side, core)),
+        (dp, place_of(level, 1 - side, core)),
+    ]
+    for hop in range(1, line):
+        partners.append((dp, place_of(lax.rem(level + hop, line), side, core)))
+    for partner in partners:
         pl.semaphore_signal(
-            barrier,
-            inc=1,
-            device_id=(other // owners, lax.rem(other, owners)),
-            device_id_type=MESH_ID,
-        )
-        return carry
-
-    lax.fori_loop(1, devices, greet, 0)
-
-    narrow_copy = pltpu.make_async_copy(narrow_hbm, narrow_buf, narrow_sem)
+            barrier, inc=1, device_id=partner, device_id_type=MESH_ID
+        )
+
+    narrow_copy = pltpu.make_async_copy(narrow_hbm, narrow_buf, small_sems.at[0])
+    count_copy = pltpu.make_async_copy(count_hbm, count_ref, small_sems.at[1])
+    late_copies = [
+        pltpu.make_async_copy(loss_hbm, loss_ref, small_sems.at[2]),
+        pltpu.make_async_copy(step_hbm, step_ref, small_sems.at[3]),
+        pltpu.make_async_copy(weight_hbm, weight_buf, small_sems.at[4]),
+        pltpu.make_async_copy(first_hbm, first_buf, small_sems.at[5]),
+        pltpu.make_async_copy(second_hbm, second_buf, small_sems.at[6]),
+    ]
     narrow_copy.start()
+    count_copy.start()
 
     def broad_copies(step):
         if step < per_half:
@@ -156,7 +191,8 @@
         for copy in broad_copies(step):
             copy.start()
 
-    live = count_ref[0]
+    count_copy.wait()
+    live = count_ref[0, 0]
     narrow_copy.wait()
     half_cols = narrow_hbm.shape[1] // 2
     slot_at = lax.broadcasted_iota(jnp.int32, (LANES, 2 * LANES), 0)
@@ -242,6 +278,8 @@
             plane_copy(2, step - per_half).start()
 
     lag = 2
+    for copy in late_copies:
+        copy.start()
     for step in range(chunks):
         if step + AHEAD < chunks:
             for copy in broad_copies(step + AHEAD):
@@ -261,12 +299,14 @@
                 step, owner % CORES, owner // CORES % SIDE, owner // (CORES * SIDE)
             ] = product[owner * SUBLANES : (owner + 1) * SUBLANES, :]
         if step == 0:
-            pl.semaphore_wait(barrier, devices - 1)
+            pl.semaphore_wait(barrier, len(partners))
         core_copy(step).start()
         if step >= lag:
             across_chip(step - lag)
     for step in range(chunks - lag, chunks):
         across_chip(step)
+    for copy in late_copies:
+        copy.wait()
 
     for item in range(per_half):
         for slot in range(3):
@@ -295,7 +335,7 @@
         jnp.where(
             lane == 1,
             live.astype(jnp.float32),
-            jnp.where(lane == 2, loss_ref[0], 0.0),
+            jnp.where(lane == 2, loss_ref[0, 0], 0.0),
         ),
     )
     stat_row[...] = row
@@ -312,6 +352,8 @@
         stat_copy(step).wait()
         return carry
 
+    first_fix = complement_power(BETA_FIRST, step_ref[0, 0])
+    second_fix = complement_power(BETA_SECOND, step_ref[0, 0])
     for step in range(chunks):
         core_copy(step).wait_send()
     for item in range(per_half):
@@ -332,37 +374,78 @@
     mean_loss = entry(2) / token_total
     clip_factor = jnp.minimum(1.0, MAX_NORM / (grad_norm + 1e-06))
     for item in range(per_half):
-        mine = pl.multiple_of((dp * per_half + item) * WIDTH, WIDTH)
-        other = pl.multiple_of(((1 - dp) * per_half + item) * WIDTH, WIDTH)
-        clipped_ref[:, pl.ds(mine, WIDTH)] = half_sum[item] / token_total * clip_factor
-        clipped_ref[:, pl.ds(other, WIDTH)] = half_in[item] / token_total * clip_factor
-    stats_ref[...] = jnp.where(lane == 0, grad_norm, mean_loss)
-
-
-def reduce_clip(groups, owners, small_cols, wide_cols, token_counts, loss_sums):
+        for source, half in ((half_sum, dp), (half_in, 1 - dp)):
+            columns = pl.ds(
+                pl.multiple_of((half * per_half + item) * WIDTH, WIDTH), WIDTH
+            )
+            clipped = source[item] / token_total * clip_factor
+            new_first = (
+                BETA_FIRST * first_buf[:, columns] + (1.0 - BETA_FIRST) * clipped
+            )
+            new_second = (
+                BETA_SECOND * second_buf[:, columns]
+                + (1.0 - BETA_SECOND) * clipped * clipped
+            )
+            first_hat = new_first / first_fix
+            second_hat = new_second / second_fix
+            weight = weight_buf[:, columns]
+            adam_step = (
+                first_hat / (jnp.sqrt(second_hat) + EPSILON_ADAM) + DECAY_RATE * weight
+            )
+            first_out[:, columns] = new_first
+            second_out[:, columns] = new_second
+            adam_out[:, columns] = adam_step
+            weight_out[:, columns] = weight - LEARN_RATE * adam_step
+    norm_out[...] = grad_norm
+    loss_out[...] = mean_loss
+
+
+def write_kernel(*refs):
+    count = len(refs) // 2
+    sems = refs[-1]
+    copies = [
+        pltpu.make_async_copy(refs[at], refs[count + at], sems.at[at])
+        for at in range(count)
+    ]
+    for copy in copies:
+        copy.start()
+    for copy in copies:
+        copy.wait()
+
+
+def on_device_kernel(
+    groups,
+    owners,
+    small_cols,
+    wide_cols,
+    token_counts,
+    loss_sums,
+    weight,
+    first_moment,
+    second_moment,
+    step,
+):
     slots, _, width = wide_cols.shape
     line = owners // (CORES * SIDE)
     chunks = width // WIDTH
     per_half = chunks // groups
     tile = (SUBLANES, WIDTH)
     dma = pltpu.SemaphoreType.DMA
-    return pl.pallas_call(
+    shapes = [weight.shape] * 4 + [(1, 1)] * 2
+    in_vmem = pl.BlockSpec(memory_space=pltpu.VMEM)
+    anywhere = pl.BlockSpec(memory_space=pl.ANY)
+    results = pl.pallas_call(
         functools.partial(reduce_kernel, groups, owners),
-        out_shape=(
-            jax.ShapeDtypeStruct((SUBLANES, width), jnp.float32),
-            jax.ShapeDtypeStruct((1, LANES), jnp.float32),
-        ),
-        in_specs=[
-            pl.BlockSpec(memory_space=pltpu.SMEM),
-            pl.BlockSpec(memory_space=pltpu.SMEM),
-            pl.BlockSpec(memory_space=pl.ANY),
-            pl.BlockSpec(memory_space=pl.ANY),
-        ],
-        out_specs=(
-            pl.BlockSpec(memory_space=pltpu.VMEM),
-            pl.BlockSpec(memory_space=pltpu.VMEM),
-        ),
+        out_shape=[pltpu.VMEM(shape, jnp.float32) for shape in shapes],
+        in_specs=[pl.BlockSpec(memory_space=pltpu.HBM)] * 8,
+        out_specs=[in_vmem] * len(shapes),
         scratch_shapes=[
+            pltpu.SMEM((1, 1), jnp.int32),
+            pltpu.SMEM((1, 1), jnp.float32),
+            pltpu.SMEM((1, 1), jnp.int32),
+            pltpu.VMEM(weight.shape, jnp.float32),
+            pltpu.VMEM(weight.shape, jnp.float32),
+            pltpu.VMEM(weight.shape, jnp.float32),
             pltpu.VMEM(small_cols.shape, jnp.bfloat16),
             pltpu.VMEM((small_cols.shape[1], 2 * slots), jnp.bfloat16),
             pltpu.VMEM((width // LANES, slots, 2, LANES), jnp.bfloat16),
@@ -376,7 +459,7 @@
             pltpu.VMEM((per_half,) + tile, jnp.float32),
             pltpu.VMEM((1, LANES), jnp.float32),
             pltpu.VMEM((groups * owners, 1, LANES), jnp.float32),
-            dma,
+            dma((7,)),
             dma((width // LANES,)),
             dma((chunks,)),
             dma((chunks,)),
@@ -390,32 +473,24 @@
             dma((groups * owners,)),
         ],
         compiler_params=pltpu.CompilerParams(collective_id=0, has_side_effects=True),
-    )(token_counts, loss_sums, small_cols, wide_cols)
-
-
-def on_device_kernel(
-    groups,
-    owners,
-    small_cols,
-    wide_cols,
-    token_counts,
-    loss_sums,
-    weight,
-    first_moment,
-    second_moment,
-    step,
-):
-    clipped, stats = reduce_clip(
-        groups, owners, small_cols, wide_cols, token_counts, loss_sums
+    )(
+        small_cols,
+        wide_cols,
+        token_counts.reshape(1, 1),
+        loss_sums.reshape(1, 1),
+        weight,
+        first_moment,
+        second_moment,
+        step.reshape(1, 1),
     )
-    new_first = BETA_FIRST * first_moment + (1.0 - BETA_FIRST) * clipped
-    new_second = BETA_SECOND * second_moment + (1.0 - BETA_SECOND) * clipped * clipped
-    step_float = step.astype(jnp.float32)
-    first_hat = new_first / (1.0 - jnp.power(jnp.float32(BETA_FIRST), step_float))
-    second_hat = new_second / (1.0 - jnp.power(jnp.float32(BETA_SECOND), step_float))
-    adam_step = first_hat / (jnp.sqrt(second_hat) + EPSILON_ADAM) + DECAY_RATE * weight
-    new_weight = weight - LEARN_RATE * adam_step
-    return (new_weight, new_first, new_second, adam_step, stats[0, 0], stats[0, 1])
+    outputs = pl.pallas_call(
+        write_kernel,
+        out_shape=[jax.ShapeDtypeStruct(shape, jnp.float32) for shape in shapes],
+        in_specs=[anywhere] * len(shapes),
+        out_specs=[anywhere] * len(shapes),
+        scratch_shapes=[dma((len(shapes),))],
+    )(*[pltpu.with_memory_space_constraint(result, pltpu.VMEM) for result in results])
+    return tuple(outputs[:4]) + (outputs[4][0, 0], outputs[5][0, 0])
 
 
 def solution(mesh):

time: 31.2 us -> 28.6 us (0.917)
  other arithmetic: 1.49 us -> 0 us
  local copies, waits for them, and re-layouts: 1.34 us -> 0 us
  Pallas kernels: 25.3 us -> 25.8 us
    sub x1 -> x0, other arithmetic: 1.49 us -> none  [on_device_kernel(): new_weight = weight - LEARN_RATE * adam_step]
    slice x1 -> x0, local copies, waits for them, and re-layouts: 1.32 us -> none  [on_device_kernel(): stats[0, 1]]
    pallas_call x1 -> x2, Pallas kernels: 25.3 us -> 25.8 us  [the longest x1 23.8 us: on_device_kernel(): pl.pallas_call(functools.partial(reduce_kernel, groups, owners), out_shap...]
where the time goes in v2:
time: 28.6 us; the launch traced here: 28.3 us
  Pallas kernels  25.8 us (90%)
  between operations  2.58 us (9%)
    pallas_call x1, Pallas kernels, on_device_kernel(): pl.pallas_call(functools.partial(reduce_kernel, groups, owners), out_shap...  23.8 us
    pallas_call x1, Pallas kernels, on_device_kernel(): pl.pallas_call(write_kernel, out_shape=[jax.ShapeDtypeStruct(shape, jnp.f...  1.99 us

profile of v2, /device:TPU:0, one launch (start us, length us, event | category | flops | bytes accessed | tf_op | source)
XLA Modules:
  0.0 28.3 jit_solution(8086518040729808539)
XLA Ops:
  2.6 23.8 %shard_map.127 = (f32[8,1536]{1,0:T(8,128)S(1)}, f32[8,1536]{1,0:T(8,128)S(1)}, f32[8,1536]{1,0:T(8,128)S(1)}, f32[8,1536]{1,0:T(8,128)S(1)}, f32[1,1]{1,0:T(1,128)}, /*index=5*/f32[1,1]{1,0:T(1,128)}) custom-call(bf16[768,128]{1,0:T(8,128)(2,1)} %narrow_hbm.1, bf16[768,2,1536]{2,1,0:T(2,128)(2,1)} %broad_hbm.1, s32[1,1]{1,0:T(1,128)} %bitcast.5.count_hbm, ...), custom_call_target="tpu_custom_call" | custom-call | tf_op jit(solution)/shard_map/pallas_call | solution.py:437
  26.4 2.0 %shard_map.128 = (f32[8,1536]{1,0:T(8,128)}, f32[8,1536]{1,0:T(8,128)}, f32[8,1536]{1,0:T(8,128)}, f32[8,1536]{1,0:T(8,128)}, f32[1,1]{1,0:T(1,128)}, /*index=5*/f32[1,1]{1,0:T(1,128)}) custom-call(f32[8,1536]{1,0:T(8,128)S(1)} %get-tuple-element.18.refs_0_, f32[8,1536]{1,0:T(8,128)S(1)} %get-tuple-element.19.refs_1_, ...), custom_call_target="tpu_custom_call" | custom-call | tf_op jit(solution)/shard_map/pallas_call | solution.py:486

commit v3 on v2

--- a/solution.py
+++ b/solution.py
@@ -111,6 +111,9 @@
     plane_in,
     plane_sum,
     line_in,
+    early_in,
+    early_sum,
+    early_plane,
     half_sum,
     half_in,
     stat_row,
@@ -123,6 +126,8 @@
     plane_recv,
     line_send,
     line_recv,
+    early_send,
+    early_recv,
     half_send,
     half_recv,
     stat_send,
@@ -187,7 +192,7 @@
             )
         return copies
 
-    for step in range(AHEAD):
+    for step in sorted(range(0, chunks, per_half))[:AHEAD]:
         for copy in broad_copies(step):
             copy.start()
 
@@ -228,8 +233,10 @@
             source, dp_to = item, 1 - dp
             side_to = side if slot == 0 else 1 - side
         return pltpu.make_async_remote_copy(
-            src_ref=chip_buf.at[source, side_to],
-            dst_ref=plane_in.at[slot, item],
+            src_ref=early_sum.at[source // per_half, side_to]
+            if item == 0
+            else chip_buf.at[source, side_to],
+            dst_ref=early_plane.at[slot] if item == 0 else plane_in.at[slot, item],
             send_sem=plane_send.at[slot, item],
             recv_sem=plane_recv.at[slot, item],
             device_id=(dp_to, place_of(level, side_to, core)),
@@ -247,6 +254,17 @@
             device_id_type=MESH_ID,
         )
 
+    def early_copy(hop, half):
+        level_to = lax.rem(level + hop, line)
+        return pltpu.make_async_remote_copy(
+            src_ref=chip_buf.at[half * per_half, :, level_to],
+            dst_ref=early_in.at[hop - 1, half],
+            send_sem=early_send.at[hop - 1, half],
+            recv_sem=early_recv.at[hop - 1, half],
+            device_id=(dp, place_of(level_to, side, core)),
+            device_id_type=MESH_ID,
+        )
+
     def half_copy():
         return pltpu.make_async_remote_copy(
             src_ref=half_sum,
@@ -271,18 +289,22 @@
     def across_chip(step):
         core_copy(step).wait_recv()
         chip_buf[step] = own_buf[step, core] + core_buf[step]
-        if step < per_half:
+        if step % per_half == 0:
+            for hop in range(line - 1, 0, -1):
+                early_copy(hop, step // per_half).start()
+        elif step < per_half:
             plane_copy(1, step).start()
             plane_copy(0, step).start()
         else:
             plane_copy(2, step - per_half).start()
 
     lag = 2
+    order = sorted(range(chunks), key=lambda at: (at % per_half != 0, at))
     for copy in late_copies:
         copy.start()
-    for step in range(chunks):
-        if step + AHEAD < chunks:
-            for copy in broad_copies(step + AHEAD):
+    for at, step in enumerate(order):
+        if at + AHEAD < chunks:
+            for copy in broad_copies(order[at + AHEAD]):
                 copy.start()
         for copy in broad_copies(step):
             copy.wait()
@@ -298,17 +320,25 @@
             own_buf[
                 step, owner % CORES, owner // CORES % SIDE, owner // (CORES * SIDE)
             ] = product[owner * SUBLANES : (owner + 1) * SUBLANES, :]
-        if step == 0:
+        if at == 0:
             pl.semaphore_wait(barrier, len(partners))
         core_copy(step).start()
-        if step >= lag:
-            across_chip(step - lag)
-    for step in range(chunks - lag, chunks):
+        if at >= lag:
+            across_chip(order[at - lag])
+    for step in order[chunks - lag :]:
         across_chip(step)
     for copy in late_copies:
         copy.wait()
 
-    for item in range(per_half):
+    for half in range(groups):
+        gathered = chip_buf[half * per_half, :, level]
+        for hop in range(1, line):
+            early_copy(hop, half).wait_recv()
+            gathered = gathered + early_in[hop - 1, half]
+        early_sum[half] = gathered
+    for slot in (1, 0, 2):
+        plane_copy(slot, 0).start()
+    for item in range(1, per_half):
         for slot in range(3):
             plane_copy(slot, item).wait_recv()
         plane_sum[item] = (
@@ -322,10 +352,16 @@
 
     squares = jnp.zeros((SUBLANES, WIDTH), jnp.float32)
     for item in range(per_half):
-        total = plane_sum[item, level]
-        for hop in range(1, line):
-            line_copy(hop, item).wait_recv()
-            total = total + line_in[hop - 1, item]
+        if item == 0:
+            total = early_sum[1, side]
+            for slot in range(3):
+                plane_copy(slot, item).wait_recv()
+                total = total + early_plane[slot]
+        else:
+            total = plane_sum[item, level]
+            for hop in range(1, line):
+                line_copy(hop, item).wait_recv()
+                total = total + line_in[hop - 1, item]
         half_sum[item] = total
         squares = squares + total * total
     lane = lax.broadcasted_iota(jnp.int32, (1, LANES), 1)
@@ -360,7 +396,10 @@
         for slot in range(3):
             plane_copy(slot, item).wait_send()
         for hop in range(1, line):
-            line_copy(hop, item).wait_send()
+            if item > 0:
+                line_copy(hop, item).wait_send()
+            if item < groups:
+                early_copy(hop, item).wait_send()
     half_copy().wait()
     lax.fori_loop(1, devices, drain_stat, 0)
 
@@ -455,6 +494,9 @@
             pltpu.VMEM((3, per_half, line) + tile, jnp.float32),
             pltpu.VMEM((per_half, line) + tile, jnp.float32),
             pltpu.VMEM((line - 1, per_half) + tile, jnp.float32),
+            pltpu.VMEM((line - 1, groups, SIDE) + tile, jnp.float32),
+            pltpu.VMEM((groups, SIDE) + tile, jnp.float32),
+            pltpu.VMEM((3,) + tile, jnp.float32),
             pltpu.VMEM((per_half,) + tile, jnp.float32),
             pltpu.VMEM((per_half,) + tile, jnp.float32),
             pltpu.VMEM((1, LANES), jnp.float32),
@@ -467,6 +509,8 @@
             dma((3, per_half)),
             dma((line - 1, per_half)),
             dma((line - 1, per_half)),
+            dma((line - 1, groups)),
+            dma((line - 1, groups)),
             dma,
             dma,
             dma((groups * owners,)),

time: 28.6 us -> 28.1 us (0.983)
  Pallas kernels: 25.8 us -> 25.3 us
    pallas_call x1, Pallas kernels: 23.8 us -> 23.3 us  [on_device_kernel(): pl.pallas_call(functools.partial(reduce_kernel, groups, owners), out_shap...]
where the time goes in v3:
time: 28.1 us; the launch traced here: 27.8 us
  Pallas kernels  25.3 us (90%)
  between operations  2.58 us (9%)
    pallas_call x1, Pallas kernels, on_device_kernel(): pl.pallas_call(functools.partial(reduce_kernel, groups, owners), out_shap...  23.3 us
    pallas_call x1, Pallas kernels, on_device_kernel(): pl.pallas_call(write_kernel, out_shape=[jax.ShapeDtypeStruct(shape, jnp.f...  1.99 us

profile of v3, /device:TPU:0, one launch (start us, length us, event | category | flops | bytes accessed | tf_op | source)
XLA Modules:
  0.0 27.8 jit_solution(16454119931820232539)
XLA Ops:
  2.6 23.3 %shard_map.127 = (f32[8,1536]{1,0:T(8,128)S(1)}, f32[8,1536]{1,0:T(8,128)S(1)}, f32[8,1536]{1,0:T(8,128)S(1)}, f32[8,1536]{1,0:T(8,128)S(1)}, f32[1,1]{1,0:T(1,128)}, /*index=5*/f32[1,1]{1,0:T(1,128)}) custom-call(bf16[768,128]{1,0:T(8,128)(2,1)} %narrow_hbm.1, bf16[768,2,1536]{2,1,0:T(2,128)(2,1)} %broad_hbm.1, s32[1,1]{1,0:T(1,128)} %bitcast.5.count_hbm, ...), custom_call_target="tpu_custom_call" | custom-call | tf_op jit(solution)/shard_map/pallas_call | solution.py:476
  25.9 2.0 %shard_map.128 = (f32[8,1536]{1,0:T(8,128)}, f32[8,1536]{1,0:T(8,128)}, f32[8,1536]{1,0:T(8,128)}, f32[8,1536]{1,0:T(8,128)}, f32[1,1]{1,0:T(1,128)}, /*index=5*/f32[1,1]{1,0:T(1,128)}) custom-call(f32[8,1536]{1,0:T(8,128)S(1)} %get-tuple-element.18.refs_0_, f32[8,1536]{1,0:T(8,128)S(1)} %get-tuple-element.19.refs_1_, ...), custom_call_target="tpu_custom_call" | custom-call | tf_op jit(solution)/shard_map/pallas_call | solution.py:530

commit v4 on v3

--- a/solution.py
+++ b/solution.py
@@ -298,7 +298,7 @@
         else:
             plane_copy(2, step - per_half).start()
 
-    lag = 2
+    lag = 1
     order = sorted(range(chunks), key=lambda at: (at % per_half != 0, at))
     for copy in late_copies:
         copy.start()

time: 28.1 us -> 28.7 us (1.021)
  Pallas kernels: 25.3 us -> 25.9 us
    pallas_call x1, Pallas kernels: 23.3 us -> 23.9 us  [on_device_kernel(): pl.pallas_call(functools.partial(reduce_kernel, groups, owners), out_shap...]
where the time goes in v4:
time: 28.7 us; the launch traced here: 28.4 us
  Pallas kernels  25.9 us (90%)
  between operations  2.58 us (9%)
    pallas_call x1, Pallas kernels, on_device_kernel(): pl.pallas_call(functools.partial(reduce_kernel, groups, owners), out_shap...  23.9 us
    pallas_call x1, Pallas kernels, on_device_kernel(): pl.pallas_call(write_kernel, out_shape=[jax.ShapeDtypeStruct(shape, jnp.f...  1.99 us

profile of v4, /device:TPU:0, one launch (start us, length us, event | category | flops | bytes accessed | tf_op | source)
XLA Modules:
  0.0 28.4 jit_solution(10254418235610905824)
XLA Ops:
  2.6 23.9 %shard_map.127 = (f32[8,1536]{1,0:T(8,128)S(1)}, f32[8,1536]{1,0:T(8,128)S(1)}, f32[8,1536]{1,0:T(8,128)S(1)}, f32[8,1536]{1,0:T(8,128)S(1)}, f32[1,1]{1,0:T(1,128)}, /*index=5*/f32[1,1]{1,0:T(1,128)}) custom-call(bf16[768,128]{1,0:T(8,128)(2,1)} %narrow_hbm.1, bf16[768,2,1536]{2,1,0:T(2,128)(2,1)} %broad_hbm.1, s32[1,1]{1,0:T(1,128)} %bitcast.5.count_hbm, ...), custom_call_target="tpu_custom_call" | custom-call | tf_op jit(solution)/shard_map/pallas_call | solution.py:476
  26.5 2.0 %shard_map.128 = (f32[8,1536]{1,0:T(8,128)}, f32[8,1536]{1,0:T(8,128)}, f32[8,1536]{1,0:T(8,128)}, f32[8,1536]{1,0:T(8,128)}, f32[1,1]{1,0:T(1,128)}, /*index=5*/f32[1,1]{1,0:T(1,128)}) custom-call(f32[8,1536]{1,0:T(8,128)S(1)} %get-tuple-element.18.refs_0_, f32[8,1536]{1,0:T(8,128)S(1)} %get-tuple-element.19.refs_1_, ...), custom_call_target="tpu_custom_call" | custom-call | tf_op jit(solution)/shard_map/pallas_call | solution.py:530
